TPU v7x, 512 devices: a whole 4x4x16 slice. The times are simulated.
512 devices in a mesh: cell: 64 (over x, z), sens: 8 (over y, core).
Axes of the slice: x: 4, y: 4, z: 16, core: 2. Of those that a mesh axis runs over, the one named last changes fastest.
Arguments:
- replicas: bfloat16 [64, 2, 64, 131072], P(None, None, 'sens', 'cell'), may hold values from -6 to 6
- csm: float32 [64, 2, 64, 64], P('cell'), as said below
Outputs:
- power: float32 [131072], P(('cell', 'sens'))
Inputs may be any that keep to these rules, and one draw needn't show every extreme that they name: For each frequency the matrix csm[f, 0] + i csm[f, 1] is Hermitian and positive definite.
All inputs are finite; a program needn't handle non-finite values.
Results may differ from a plain program's by a relative error of at most 0.00035.
Values may be sent and summed in bfloat16 or wider, within the bound.
A program may use at most 64 MiB of HBM per device.

v0:
```python
import functools

import jax
import jax.numpy as jnp
from jax import lax
from jax.sharding import Mesh
from jax.sharding import PartitionSpec as P

CELL = ("cell_0", "cell_1")
SENS = ("sens_0", "sens_1")
CELL_SENS = ("cell_0", "cell_1", "sens_0", "sens_1")


def joined_along(parts, dim):
    parts = jnp.moveaxis(parts, 0, dim)
    lengths = parts.shape
    return parts.reshape(*lengths[:dim], lengths[dim] * lengths[dim + 1], *lengths[dim + 2 :])


def all_blocks(value, axes, order):
    parts = value
    for k in order:
        parts = lax.all_gather(parts, axes[k])
    done = order[::-1]
    back = [done.index(k) for k in range(len(axes))]
    parts = parts.transpose(*back, *range(len(axes), parts.ndim))
    return parts.reshape(-1, *value.shape)


def whole_of(value, axes, order, dim):
    return joined_along(all_blocks(value, axes, order), dim)


def cut_along(value, dim, peers):
    before, after = (value.shape[:dim], value.shape[dim + 1 :])
    return jnp.moveaxis(value.reshape(*before, peers, -1, *after), dim, 0)


def sent_and_summed(value, axis, dim):
    parts = cut_along(value, dim, lax.axis_size(axis))
    arrived = lax.all_to_all(parts, axis, split_axis=0, concat_axis=0, tiled=True)
    return arrived.sum(axis=0)


def one_axis_at_a_time(value, axes):
    return functools.reduce(lax.pmax, axes, value)


def band_power(scaled, waves):
    real_k = scaled[:, 0]
    imag_k = scaled[:, 1]
    real_w = waves[:, 0]
    imag_w = waves[:, 1]
    real_y = jnp.einsum(
        "fst,ftc->fsc", real_k, real_w, preferred_element_type=jnp.float32
    ) - jnp.einsum("fst,ftc->fsc", imag_k, imag_w, preferred_element_type=jnp.float32)
    imag_y = jnp.einsum(
        "fst,ftc->fsc", real_k, imag_w, preferred_element_type=jnp.float32
    ) + jnp.einsum("fst,ftc->fsc", imag_k, real_w, preferred_element_type=jnp.float32)
    real_f = real_w.astype(jnp.float32)
    imag_f = imag_w.astype(jnp.float32)
    numer = jnp.sum(real_f * real_y + imag_f * imag_y, axis=1)
    denom = jnp.sum(real_f * real_f + imag_f * imag_f, axis=1)
    return jnp.sum(numer / denom, axis=0)


def shards(replicas, csm):
    spectra = whole_of(csm.astype(jnp.bfloat16), CELL, (0, 1), 0).astype(csm.dtype)
    trace = jnp.sum(jnp.diagonal(spectra[:, 0], axis1=1, axis2=2), axis=1)
    scaled = (spectra / trace[:, None, None, None]).astype(jnp.bfloat16)
    waves = lax.all_to_all(replicas, SENS, split_axis=0, concat_axis=2, tiled=True)
    count = waves.shape[0]
    mine = lax.dynamic_slice_in_dim(scaled, lax.axis_index(SENS) * count, count, 0)
    partial_value = band_power(mine, waves)
    total = sent_and_summed(partial_value, SENS, 0)
    highest = one_axis_at_a_time(jnp.max(total), CELL_SENS)
    return total / highest


def solution(mesh):
    finer = Mesh(mesh.devices.reshape(4, 16, 4, 2), ("cell_0", "cell_1", "sens_0", "sens_1"))
    return jax.shard_map(
        shards,
        mesh=finer,
        in_specs=(P(None, None, SENS, CELL), P(CELL, None, None, None)),
        out_specs=P(CELL_SENS),
        check_vma=False,
    )
```

profile of v0, /device:TPU:1, one launch (start us, length us, event | category | flops | bytes accessed | tf_op | source)
XLA Modules:
  0.0 191.3 jit_solution(1041722249178385859)
XLA Ops:
  6.5 0.0 copy-start.1
  6.5 11.4 %all-to-all-start = ((bf16[64,2,8,2048]{3,2,1,0:T(8,128)(2,1)}), bf16[64,2,8,2048]{3,2,1,0:T(8,128)(2,1)}, u32[]{:S(2)}, u32[]{:S(2)}) async-start(bf16[64,2,8,2048]{3,2,1,0:T(8,128)(2,1)} %param.2), calls=%async_computation | async-start | bytes 8388608 | tf_op jit(solution)/shard_map/all_to_all | solution.py:71
  17.9 0.0 all-gather.4.cloned.1.call-start
  17.9 0.0 copy-done.1
  17.9 10.7 %all-gather = bf16[4,2,64,64]{3,2,1,0:T(8,128)(2,1)} all-gather(bf16[1,2,64,64]{3,2,1,0:T(8,128)(2,1)S(1)} %convert_element_type.22), channel_id=2, replica_groups=mesh['cell_0'=4,'cell_1'=16,'sens_0'=4,'sens_1'=2] {'cell_0'}, dimensions={0}, use_global_device_ids=true | all-gather | bytes 81920 | tf_op jit(solution)/shard_map/all_gather | solution.py:23
  28.7 0.0 all-gather.4.cloned.1.call-update
  28.7 64.8 %all-gather.4.cloned.1.call-done = bf16[64,2,64,64]{3,2,1,0:T(8,128)(2,1)} async-done(((bf16[4,2,64,64]{3,2,1,0:T(8,128)(2,1)}), bf16[64,2,64,64]{3,2,1,0:T(8,128)(2,1)}) %all-gather.4.cloned.1.call-update) | async-done | bytes 1048592 | tf_op jit(solution)/shard_map/all_gather | solution.py:23
  93.5 2.0 %copy.13 = f32[16,4,1,2,64,64]{5,4,0,1,3,2:T(8,128)S(1)} copy(bf16[16,4,1,2,64,64]{5,4,3,1,0,2:T(8,128)(2,1)} %bitcast.48) | data formatting | bytes 3145728 | tf_op jit(solution)/shard_map/convert_element_type | solution.py:68
  95.5 0.0 copy-start
  95.6 2.0 %copy-done = f32[16,4,1,2,64,64]{5,4,0,1,3,2:T(8,128)} copy-done((f32[16,4,1,2,64,64]{5,4,0,1,3,2:T(8,128)}, f32[16,4,1,2,64,64]{5,4,0,1,3,2:T(8,128)S(1)}, u32[]{:S(2)}) %copy-start) | copy-done | bytes 2097176
  97.5 0.1 slice_bitcast_fusion.1
  97.7 2.2 %copy.14 = f32[64,64,64]{0,2,1:T(8,128)} copy(f32[64,64,64]{2,1,0:T(8,128)S(1)} %slice_bitcast_fusion.1) | data formatting | bytes 2097152 | tf_op jit(solution)/shard_map/squeeze | solution.py:69
  99.9 1.5 gather_fusion
  101.4 0.1 dynamic-slice
  101.5 1.2 fusion.7
  102.6 0.0 all-to-all-done
  102.6 2.7 %copy.19 = bf16[8,8,2,8,2048]{4,3,0,1,2:T(8,128)(2,1)S(1)} copy(bf16[8,8,2,8,2048]{4,3,2,1,0:T(8,128)(2,1)} %bitcast) | data formatting | bytes 8388608 | tf_op jit(solution)/shard_map/all_to_all | solution.py:71
  105.4 0.7 fusion.6
  106.1 0.7 fusion.4
  106.8 0.7 fusion.5
  107.4 0.9 fusion.3
  108.4 1.9 fusion.1
  110.3 18.0 %all_to_all.27 = f32[8,1,256]{2,1,0:T(1,128)S(1)} all-to-all(f32[8,1,256]{2,1,0:T(1,128)S(1)} %bitcast.49), channel_id=1, replica_groups=mesh['cell_0'=4,'cell_1'=16,'sens_0'=4,'sens_1'=2] {'sens_0','sens_1'}, dimensions={0} | all-to-all | bytes 16384 | tf_op jit(solution)/shard_map/all_to_all | solution.py:41
  128.3 0.6 reduce_max.9
  128.9 8.9 %pmax.28 = f32[]{:T(128)} all-reduce(f32[]{:T(128)} %reduce_max.9), channel_id=1, replica_groups=mesh['cell_0'=4,'cell_1'=16,'sens_0'=4,'sens_1'=2] {'cell_0'}, use_global_device_ids=true, to_apply=%region_6.7 | all-reduce | flops 1 | bytes 8 | tf_op jit(solution)/shard_map/pmax | solution.py:46
  137.8 23.2 %pmax.29 = f32[]{:T(128)} all-reduce(f32[]{:T(128)} %pmax.28), channel_id=1, replica_groups=mesh['cell_0'=4,'cell_1'=16,'sens_0'=4,'sens_1'=2] {'cell_1'}, use_global_device_ids=true, to_apply=%region_7.8 | all-reduce | flops 1 | bytes 8 | tf_op jit(solution)/shard_map/pmax | solution.py:46
  161.0 7.5 %pmax.30 = f32[]{:T(128)} all-reduce(f32[]{:T(128)} %pmax.29), channel_id=1, replica_groups=mesh['cell_0'=4,'cell_1'=16,'sens_0'=4,'sens_1'=2] {'sens_0'}, use_global_device_ids=true, to_apply=%region_8.9 | all-reduce | flops 1 | bytes 8 | tf_op jit(solution)/shard_map/pmax | solution.py:46
  168.4 14.8 %pmax.31 = f32[]{:T(128)} all-reduce(f32[]{:T(128)} %pmax.30), channel_id=1, replica_groups=mesh['cell_0'=4,'cell_1'=16,'sens_0'=4,'sens_1'=2] {'sens_1'}, use_global_device_ids=true, to_apply=%region_9.10 | all-reduce | flops 1 | bytes 8 | tf_op jit(solution)/shard_map/pmax | solution.py:46
  183.2 1.3 broadcast_divide_fusion
  (5 shorter events, 0.1 us)
Async XLA Ops:
  6.5 11.4 %copy-start.1 = (f32[1,2,64,64]{3,2,1,0:T(8,128)S(1)}, f32[1,2,64,64]{3,2,1,0:T(8,128)}, u32[]{:S(2)}) copy-start(f32[1,2,64,64]{3,2,1,0:T(8,128)} %param.3) | copy-start | bytes 98308
  6.5 96.1 %all-to-all-start = ((bf16[64,2,8,2048]{3,2,1,0:T(8,128)(2,1)}), bf16[64,2,8,2048]{3,2,1,0:T(8,128)(2,1)}, u32[]{:S(2)}, u32[]{:S(2)}) async-start(bf16[64,2,8,2048]{3,2,1,0:T(8,128)(2,1)} %param.2), calls=%async_computation | async-start | bytes 8388608 | tf_op jit(solution)/shard_map/all_to_all | solution.py:71
  17.9 75.6 %all-gather.4.cloned.1.call-start = ((), (), s32[]{:S(2)}) async-start(), calls=%async_computation.2 | async-start | bytes 2228224 | tf_op jit(solution)/shard_map/all_gather | solution.py:23
  95.5 2.0 %copy-start = (f32[16,4,1,2,64,64]{5,4,0,1,3,2:T(8,128)}, f32[16,4,1,2,64,64]{5,4,0,1,3,2:T(8,128)S(1)}, u32[]{:S(2)}) copy-start(f32[16,4,1,2,64,64]{5,4,0,1,3,2:T(8,128)S(1)} %copy.13) | copy-start | bytes 6291460
Sparse Core Ops, SparseCore 0:
  28.8 64.6 all-gather.3
where the time goes:
time: 192 us; the launch traced here: 191 us
  blocking collectives  83 us (43%)
  waiting for transfers between devices  64.8 us (34%)
  between operations  13.5 us (7%)
  starting transfers between devices  11.4 us (6%)
  local copies, waits for them, and re-layouts  10.6 us (6%)
  other arithmetic  4.06 us (2%)
  matrix products  3.92 us (2%)
    all_gather x1, waiting for transfers between devices, all_blocks(): parts = lax.all_gather(parts, axes[k])  64.8 us
    pmax x4, blocking collectives, one_axis_at_a_time(): return functools.reduce(lax.pmax, axes, value)  54.4 us
    all_to_all x1, blocking collectives, sent_and_summed(): lax.all_to_all(parts, axis, split_axis=0, concat_axis=0, tiled=True)  18 us
    all_to_all x1, starting transfers between devices, shards(): lax.all_to_all(replicas, SENS, split_axis=0, concat_axis=2, tiled=True)  11.4 us
    all_gather x1, blocking collectives, all_blocks(): parts = lax.all_gather(parts, axes[k])  10.7 us
  transfers between devices with their start and end apart: 2, of which 1 were waited for; matrix products, arithmetic and copies ran while one was open for 4% of the time, Pallas kernels for 0%

commit v1 on v0

v1 whole, which is shorter than its diff:
```python
import functools

import jax
import jax.numpy as jnp
from jax import lax
from jax.experimental import pallas as pl
from jax.experimental.pallas import tpu as pltpu
from jax.sharding import Mesh
from jax.sharding import PartitionSpec as P

MESH = pl.DeviceIdType.MESH
CELL = ("cx", "cz")
SENS = ("sy", "sc")
ALL = ("cx", "cz", "sy", "sc")

CHUNKS = 8


def kernel(
    sizes,
    waves_hbm,
    csm_hbm,
    out_ref,
    csm_vmem,
    waves,
    mats,
    peak_s,
    peak_z,
    peak_x,
    local_sem,
    wave_send,
    wave_recv,
    z_send,
    z_recv,
    x_send,
    x_recv,
    ps_send,
    ps_recv,
    pz_send,
    pz_recv,
    px_send,
    px_recv,
):
    nx, nz, ny, nc = sizes
    ns = ny * nc
    cx, cz = lax.axis_index("cx"), lax.axis_index("cz")
    sy, sc = lax.axis_index("sy"), lax.axis_index("sc")
    me = sy * nc + sc
    freqs, _, rows, _ = waves_hbm.shape
    cells = waves.shape[-1]
    step = freqs // CHUNKS

    def at_s(s):
        return {"cx": cx, "cz": cz, "sy": s // nc, "sc": s % nc}

    def at_z(z):
        return {"cx": cx, "cz": z, "sy": sy, "sc": sc}

    def at_x(x):
        return {"cx": x, "cz": cz, "sy": sy, "sc": sc}

    sens_peers = [lax.rem(me + i, ns) for i in range(1, ns)]
    z_peers = [lax.rem(cz + i, nz) for i in range(1, nz)]
    x_peers = [lax.rem(cx + i, nx) for i in range(1, nx)]

    csm_in = pltpu.make_async_copy(csm_hbm.at[0], csm_vmem, local_sem.at[0])
    csm_in.start()

    def own_block(s):
        return pl.ds(pl.multiple_of(s * cells, cells), cells)

    keep = pltpu.make_async_copy(waves_hbm.at[:, :, :, own_block(me)], waves.at[me], local_sem.at[1])
    keep.start()

    barrier = pltpu.get_barrier_semaphore()
    for s in sens_peers:
        pl.semaphore_signal(barrier, inc=1, device_id=at_s(s), device_id_type=MESH)
    for x in x_peers:
        pl.semaphore_signal(barrier, inc=1, device_id=at_x(x), device_id_type=MESH)
    for z in z_peers:
        pl.semaphore_signal(barrier, inc=1, device_id=at_z(z), device_id_type=MESH)

    csm_in.wait()
    real, imag = csm_vmem[0], csm_vmem[1]
    side = real.shape[0]
    diag = lax.broadcasted_iota(jnp.int32, (side, side), 0) == lax.broadcasted_iota(jnp.int32, (side, side), 1)
    trace = jnp.sum(jnp.where(diag, real, 0.0))
    mats[cx, cz] = jnp.concatenate([real / trace, imag / trace], axis=1).astype(jnp.bfloat16)

    pl.semaphore_wait(barrier, len(sens_peers) + len(x_peers) + len(z_peers))

    def wave_copy(chunk, i, to, frm):
        part = pl.ds(chunk * step, step)
        return pltpu.make_async_remote_copy(
            src_ref=waves_hbm.at[part, :, :, own_block(to)],
            dst_ref=waves.at[frm, part],
            send_sem=wave_send.at[chunk, i],
            recv_sem=wave_recv.at[chunk, i],
            device_id=at_s(to),
            device_id_type=MESH,
        )

    for chunk in range(CHUNKS):
        for i, s in enumerate(sens_peers):
            wave_copy(chunk, i, s, me).start()

    def z_copy(i, to, frm):
        return pltpu.make_async_remote_copy(
            src_ref=mats.at[cx, frm],
            dst_ref=mats.at[cx, frm],
            send_sem=z_send.at[i],
            recv_sem=z_recv.at[i],
            device_id=at_z(to),
            device_id_type=MESH,
        )

    def x_copy(i, to, frm):
        return pltpu.make_async_remote_copy(
            src_ref=mats.at[frm],
            dst_ref=mats.at[frm],
            send_sem=x_send.at[i],
            recv_sem=x_recv.at[i],
            device_id=at_x(to),
            device_id_type=MESH,
        )

    for i, z in enumerate(z_peers):
        z_copy(i, z, cz).start()
    for i, z in enumerate(z_peers):
        z_copy(i, z, lax.rem(cz + nz - 1 - i, nz)).wait_recv()
    for i, x in enumerate(x_peers):
        x_copy(i, x, cx).start()
    for i, x in enumerate(x_peers):
        x_copy(i, x, lax.rem(cx + nx - 1 - i, nx)).wait_recv()
    keep.wait()

    lane = lax.broadcasted_iota(jnp.int32, (side, 2 * side), 1)
    sign = jnp.where(lane < side, 1.0, -1.0)

    def term(f):
        fields = [waves[s, f, h].astype(jnp.float32) for h in range(2) for s in range(ns)]
        w = jnp.concatenate(fields, axis=0)
        a = mats[f // nz, f % nz].astype(jnp.float32)
        b = jnp.concatenate([a * sign, pltpu.roll(a, side, 1)], axis=0).astype(jnp.bfloat16)
        y = jnp.dot(b, w.astype(jnp.bfloat16), preferred_element_type=jnp.float32)
        numer = jnp.sum(w * y, axis=0, keepdims=True)
        denom = jnp.sum(w * w, axis=0, keepdims=True)
        return numer / denom

    total = jnp.zeros((1, cells), jnp.float32)
    for chunk in range(CHUNKS):
        for i, s in enumerate(sens_peers):
            wave_copy(chunk, i, s, lax.rem(me + ns - 1 - i, ns)).wait_recv()
        total = lax.fori_loop(chunk * step, (chunk + 1) * step, lambda f, t: t + term(f), total)

    def highest_of(value, buf, send, recv, peers, at, mine, count):
        buf[mine] = value

        def copy(i, to, frm):
            return pltpu.make_async_remote_copy(
                src_ref=buf.at[frm],
                dst_ref=buf.at[frm],
                send_sem=send.at[i],
                recv_sem=recv.at[i],
                device_id=at(to),
                device_id_type=MESH,
            )

        for i, p in enumerate(peers):
            copy(i, p, mine).start()
        for i, p in enumerate(peers):
            copy(i, p, lax.rem(mine + count - 1 - i, count)).wait_recv()
        for i, p in enumerate(peers):
            copy(i, p, mine).wait_send()
        return jnp.max(buf[...], axis=0)

    lanes = peak_s.shape[-1]
    peak = functools.reduce(jnp.maximum, [total[:, k : k + lanes] for k in range(0, cells, lanes)])
    peak = highest_of(peak, peak_s, ps_send, ps_recv, sens_peers, at_s, me, ns)
    peak = highest_of(peak, peak_z, pz_send, pz_recv, z_peers, at_z, cz, nz)
    peak = highest_of(peak, peak_x, px_send, px_recv, x_peers, at_x, cx, nx)
    out_ref[...] = total / jnp.max(peak)

    for chunk in range(CHUNKS):
        for i, s in enumerate(sens_peers):
            wave_copy(chunk, i, s, me).wait_send()
    for i, z in enumerate(z_peers):
        z_copy(i, z, cz).wait_send()
    for i, x in enumerate(x_peers):
        x_copy(i, x, cx).wait_send()


def solution(mesh):
    sizes = (4, 16, 4, 2)
    finer = Mesh(mesh.devices.reshape(sizes), ALL)
    nx, nz, ny, nc = sizes
    ns = ny * nc

    def shards(waves, csm):
        freqs, _, rows, wide = waves.shape
        side = csm.shape[-1]
        cells = wide // ns
        dma = pltpu.SemaphoreType.DMA
        out = pl.pallas_call(
            functools.partial(kernel, sizes),
            out_shape=jax.ShapeDtypeStruct((1, cells), jnp.float32),
            in_specs=[pl.BlockSpec(memory_space=pl.ANY)] * 2,
            out_specs=pl.BlockSpec(memory_space=pltpu.VMEM),
            scratch_shapes=[
                pltpu.VMEM((2, side, side), jnp.float32),
                pltpu.VMEM((ns, freqs, 2, rows, cells), jnp.bfloat16),
                pltpu.VMEM((nx, nz, side, 2 * side), jnp.bfloat16),
                pltpu.VMEM((ns, 1, 128), jnp.float32),
                pltpu.VMEM((nz, 1, 128), jnp.float32),
                pltpu.VMEM((nx, 1, 128), jnp.float32),
                dma((2,)),
                dma((CHUNKS, ns - 1)),
                dma((CHUNKS, ns - 1)),
                dma((nz - 1,)),
                dma((nz - 1,)),
                dma((nx - 1,)),
                dma((nx - 1,)),
                dma((ns - 1,)),
                dma((ns - 1,)),
                dma((nz - 1,)),
                dma((nz - 1,)),
                dma((nx - 1,)),
                dma((nx - 1,)),
            ],
            compiler_params=pltpu.CompilerParams(collective_id=0, has_side_effects=True),
        )(waves, csm)
        return out.reshape(cells)

    return jax.shard_map(
        shards,
        mesh=finer,
        in_specs=(P(None, None, SENS, CELL), P(CELL, None, None, None)),
        out_specs=P(ALL),
        check_vma=False,
    )
```

time: 192 us -> 80.6 us (0.42)
  blocking collectives: 83 us -> 0 us
  Pallas kernels: 0 us -> 79.2 us
  waiting for transfers between devices: 64.8 us -> 0 us
  between operations: 13.5 us -> 0.01 us
  starting transfers between devices: 11.4 us -> 0 us
  local copies, waits for them, and re-layouts: 10.6 us -> 1.24 us
  other arithmetic: 4.06 us -> 0 us
  matrix products: 3.92 us -> 0 us
    pallas_call x0 -> x1, Pallas kernels: none -> 79.2 us  [shards(): pl.pallas_call(functools.partial(kernel, sizes), out_shape=jax.ShapeDtype...]
    all_gather x1 -> x0, waiting for transfers between devices: 64.8 us -> none  [all_blocks(): parts = lax.all_gather(parts, axes[k])]
    pmax x4 -> x0, blocking collectives: 54.4 us -> none  [one_axis_at_a_time(): return functools.reduce(lax.pmax, axes, value)]
    all_to_all x1 -> x0, blocking collectives: 18 us -> none  [sent_and_summed(): lax.all_to_all(parts, axis, split_axis=0, concat_axis=0, tiled=True)]
    all_to_all x1 -> x0, starting transfers between devices: 11.4 us -> none  [shards(): lax.all_to_all(replicas, SENS, split_axis=0, concat_axis=2, tiled=True)]
    all_gather x1 -> x0, blocking collectives: 10.7 us -> none  [all_blocks(): parts = lax.all_gather(parts, axes[k])]
    dot_general x4 -> x0, matrix products: 3.92 us -> none  [the longest x1 1.86 us: band_power(): jnp.einsum('fst,ftc->fsc', imag_k, real_w, preferred_element_type=jnp.flo...]
    all_to_all x1 -> x0, local copies, waits for them, and re-layouts: 2.71 us -> none  [shards(): lax.all_to_all(replicas, SENS, split_axis=0, concat_axis=2, tiled=True)]
  transfers between devices with their start and end apart: 2 -> 0, of which waited for: 1 -> 0; matrix products, arithmetic and copies ran while one was open for 4% -> 0% of each run, Pallas kernels for 0% -> 0%
where the time goes in v1:
time: 80.6 us; the launch traced here: 80.4 us
  Pallas kernels  79.2 us (98%)
  local copies, waits for them, and re-layouts  1.24 us (2%)
    pallas_call x1, Pallas kernels, shards(): pl.pallas_call(functools.partial(kernel, sizes), out_shape=jax.ShapeDtype...  79.2 us

profile of v1, /device:TPU:1, one launch (start us, length us, event | category | flops | bytes accessed | tf_op | source)
XLA Modules:
  0.0 80.4 jit_solution(14550305938836922302)
XLA Ops:
  0.0 79.2 %shard_map.28 = f32[1,256]{1,0:T(1,128)} custom-call(bf16[64,2,8,2048]{3,2,1,0:T(8,128)(2,1)} %waves_hbm.1, f32[1,2,64,64]{3,2,1,0:T(8,128)} %csm_hbm.1), custom_call_target="tpu_custom_call" | custom-call | tf_op jit(solution)/shard_map/pallas_call | solution.py:204
  79.2 1.2 %copy.4 = f32[256]{0:T(256)} copy(f32[256]{0:T(256)} %bitcast.1) | data formatting | bytes 2048

commit v2 on v0

v2 whole, which is shorter than its diff:
```python
import functools

import jax
import jax.numpy as jnp
from jax import lax
from jax.experimental import pallas as pl
from jax.experimental.pallas import tpu as pltpu
from jax.sharding import Mesh
from jax.sharding import PartitionSpec as P

MESH = pl.DeviceIdType.MESH
CELL = ("cx", "cz")
SENS = ("sy", "sc")
ALL = ("cx", "cz", "sy", "sc")
SIZES = (4, 16, 4, 2)

CHUNKS = (56, 8)
UNROLL = 8
LANES = 128

NX, NZ, NY, NC = SIZES
NS = NY * NC
NEAR = [(0, 0, c, d) for c in range(NY) for d in range(NC)]
ALONG_X = [(a, 0, 0, 0) for a in range(NX)]
ALONG_Z = [(0, b, 0, 0) for b in range(NZ)]
PLANE = [(a, 0, c, d) for a in range(NX) for c in range(NY) for d in range(NC)]
PHASES = (PLANE, ALONG_Z)


def opposite(offset):
    return tuple((n - v) % n for n, v in zip(SIZES, offset))


def far_first(offsets):
    return sorted(offsets[1:], key=lambda o: -sum(min(v, n - v) for n, v in zip(SIZES, o)))


def kernel(
    waves_hbm,
    csm_hbm,
    out_ref,
    csm_vmem,
    waves,
    mats,
    local_sem,
    wave_send,
    wave_recv,
    ring_send,
    ring_recv,
    x_send,
    x_recv,
    *peak_refs,
):
    place = [lax.axis_index(name) for name in ALL]
    cx, cz, sy, sc = place
    me = sy * NC + sc
    freqs = waves.shape[1]
    cells = waves.shape[-1]
    starts = [sum(CHUNKS[:k]) for k in range(len(CHUNKS))]

    def at(offset):
        return {name: p if o == 0 else lax.rem(p + o, n) for name, p, o, n in zip(ALL, place, offset, SIZES)}

    csm_in = pltpu.make_async_copy(csm_hbm.at[0], csm_vmem, local_sem.at[0])
    csm_in.start()

    barrier = pltpu.get_barrier_semaphore()
    greeted = NEAR[1:] + ALONG_X[1:] + [ALONG_Z[1], ALONG_Z[-1]]
    for offset in greeted:
        pl.semaphore_signal(barrier, inc=1, device_id=at(offset), device_id_type=MESH)

    csm_in.wait()
    real, imag = csm_vmem[0], csm_vmem[1]
    side = real.shape[0]
    diag = lax.broadcasted_iota(jnp.int32, (side, side), 0) == lax.broadcasted_iota(jnp.int32, (side, side), 1)
    trace = jnp.sum(jnp.where(diag, real, 0.0))
    mats[cx, cz] = jnp.concatenate([real / trace, imag / trace], axis=1).astype(jnp.bfloat16)

    pl.semaphore_wait(barrier, len(greeted))

    def block(s):
        return pl.ds(pl.multiple_of(s * cells, cells), cells)

    def wave_copy(chunk, offset):
        part = pl.ds(starts[chunk], CHUNKS[chunk])
        i = NEAR.index(offset)
        to = at(offset)
        return pltpu.make_async_remote_copy(
            src_ref=waves_hbm.at[part, :, :, block(to["sy"] * NC + to["sc"])],
            dst_ref=waves.at[me, part],
            send_sem=wave_send.at[chunk, i],
            recv_sem=wave_recv.at[chunk, me],
            device_id=to,
            device_id_type=MESH,
        )

    def wave_arrival(chunk, s):
        part = pl.ds(starts[chunk], CHUNKS[chunk])
        return pltpu.make_async_remote_copy(
            src_ref=waves_hbm.at[part, :, :, block(s)],
            dst_ref=waves.at[s, part],
            send_sem=wave_send.at[chunk, 0],
            recv_sem=wave_recv.at[chunk, s],
            device_id=at(NEAR[1]),
            device_id_type=MESH,
        )

    def own_copy():
        return pltpu.make_async_copy(waves_hbm.at[:, :, :, block(me)], waves.at[me], local_sem.at[1])

    for chunk in range(len(CHUNKS)):
        for offset in far_first(NEAR):
            wave_copy(chunk, offset).start()
    own_copy().start()

    def ring_copy(way, hop):
        here = lax.rem(cz + (NZ - hop + 1 if way == 0 else hop - 1), NZ)
        return pltpu.make_async_remote_copy(
            src_ref=mats.at[cx, here],
            dst_ref=mats.at[cx, here],
            send_sem=ring_send.at[way, hop],
            recv_sem=ring_recv.at[way, hop],
            device_id=at(ALONG_Z[1] if way == 0 else ALONG_Z[-1]),
            device_id_type=MESH,
        )

    def ring_arrival(way, hop):
        here = lax.rem(cz + (NZ - hop if way == 0 else hop), NZ)
        return pltpu.make_async_remote_copy(
            src_ref=mats.at[cx, here],
            dst_ref=mats.at[cx, here],
            send_sem=ring_send.at[way, hop],
            recv_sem=ring_recv.at[way, hop],
            device_id=at(ALONG_Z[1]),
            device_id_type=MESH,
        )

    def x_copy(offset):
        i = ALONG_X.index(offset)
        return pltpu.make_async_remote_copy(
            src_ref=mats.at[cx],
            dst_ref=mats.at[cx],
            send_sem=x_send.at[i],
            recv_sem=x_recv.at[cx],
            device_id=at(offset),
            device_id_type=MESH,
        )

    def x_arrival(offset):
        x = at(offset)["cx"]
        return pltpu.make_async_remote_copy(
            src_ref=mats.at[x],
            dst_ref=mats.at[x],
            send_sem=x_send.at[0],
            recv_sem=x_recv.at[x],
            device_id=at(ALONG_X[1]),
            device_id_type=MESH,
        )

    hops = [(0, h) for h in range(1, NZ // 2 + 1)] + [(1, h) for h in range(1, (NZ + 1) // 2)]
    hops.sort(key=lambda wh: wh[1])
    for way, hop in hops:
        if hop == 1:
            ring_copy(way, hop).start()
    for way, hop in hops:
        ring_arrival(way, hop).wait_recv()
        if (way, hop + 1) in hops:
            ring_copy(way, hop + 1).start()
    for offset in ALONG_X[1:]:
        x_copy(offset).start()
    for offset in ALONG_X[1:]:
        x_arrival(offset).wait_recv()
    own_copy().wait()

    lane = lax.broadcasted_iota(jnp.int32, (side, 2 * side), 1)
    sign = jnp.where(lane < side, 1.0, -1.0)

    def term(f):
        fields = [waves[s, f, h].astype(jnp.float32) for h in range(2) for s in range(NS)]
        w = jnp.concatenate(fields, axis=0).astype(jnp.bfloat16)
        a = mats[f // NZ, f % NZ].astype(jnp.float32)
        b = jnp.concatenate([a * sign, pltpu.roll(a, side, 1)], axis=0).astype(jnp.bfloat16)
        y = jnp.dot(b, w, preferred_element_type=jnp.float32)
        rows = fields[0].shape[0]
        numer = functools.reduce(jnp.add, [v * y[k * rows : (k + 1) * rows] for k, v in enumerate(fields)])
        denom = functools.reduce(jnp.add, [v * v for v in fields])
        return jnp.sum(numer, axis=0, keepdims=True) / jnp.sum(denom, axis=0, keepdims=True)

    total = jnp.zeros((1, cells), jnp.float32)
    for chunk, first in enumerate(starts):
        for offset in far_first(NEAR)[::-1]:
            s = at(offset)
            wave_arrival(chunk, s["sy"] * NC + s["sc"]).wait_recv()
        count = CHUNKS[chunk]
        total = lax.fori_loop(first, first + count, lambda f, t: t + term(f), total, unroll=min(UNROLL, count))

    def peak_copies(phase):
        offsets = PHASES[phase]
        slots, send, recv = peak_refs[3 * phase : 3 * phase + 3]

        def copy(offset):
            i, back = offsets.index(offset), offsets.index(opposite(offset))
            return pltpu.make_async_remote_copy(
                src_ref=slots.at[0],
                dst_ref=slots.at[back],
                send_sem=send.at[i],
                recv_sem=recv.at[back],
                device_id=at(offset),
                device_id_type=MESH,
            )

        return slots, [copy(o) for o in far_first(offsets)]

    peak = functools.reduce(jnp.maximum, [total[:, k : k + LANES] for k in range(0, cells, LANES)])
    for phase in range(len(PHASES)):
        slots, copies = peak_copies(phase)
        slots[0] = peak
        for copy in copies:
            copy.start()
        for offset in far_first(PHASES[phase])[::-1]:
            i = PHASES[phase].index(offset)
            _, send, recv = peak_refs[3 * phase : 3 * phase + 3]
            pltpu.make_async_remote_copy(
                src_ref=slots.at[0],
                dst_ref=slots.at[i],
                send_sem=send.at[i],
                recv_sem=recv.at[i],
                device_id=at(offset),
                device_id_type=MESH,
            ).wait_recv()
        peak = jnp.max(slots[...], axis=0)
    out_ref[...] = total / jnp.max(peak)

    for chunk in range(len(CHUNKS)):
        for offset in NEAR[1:]:
            wave_copy(chunk, offset).wait_send()
    for way, hop in hops:
        ring_copy(way, hop).wait_send()
    for offset in ALONG_X[1:]:
        x_copy(offset).wait_send()
    for phase in range(len(PHASES)):
        for copy in peak_copies(phase)[1]:
            copy.wait_send()


def solution(mesh):
    finer = Mesh(mesh.devices.reshape(SIZES), ALL)

    def shards(waves, csm):
        freqs, _, rows, wide = waves.shape
        side = csm.shape[-1]
        cells = wide // NS
        dma = pltpu.SemaphoreType.DMA
        peaks = [s for p in PHASES for s in (pltpu.VMEM((len(p), 1, LANES), jnp.float32), dma((len(p),)), dma((len(p),)))]
        out = pl.pallas_call(
            kernel,
            out_shape=pltpu.VMEM((1, cells), jnp.float32),
            in_specs=[pl.BlockSpec(memory_space=pl.ANY)] * 2,
            out_specs=pl.BlockSpec(memory_space=pltpu.VMEM),
            scratch_shapes=[
                pltpu.VMEM((2, side, side), jnp.float32),
                pltpu.VMEM((NS, freqs, 2, rows, cells), jnp.bfloat16),
                pltpu.VMEM((NX, NZ, side, 2 * side), jnp.bfloat16),
                dma((2,)),
                dma((len(CHUNKS), NS)),
                dma((len(CHUNKS), NS)),
                dma((2, NZ // 2 + 1)),
                dma((2, NZ // 2 + 1)),
                dma((NX,)),
                dma((NX,)),
                *peaks,
            ],
            compiler_params=pltpu.CompilerParams(collective_id=0, has_side_effects=True),
        )(waves, csm)
        return out.reshape(cells)

    return jax.shard_map(
        shards,
        mesh=finer,
        in_specs=(P(None, None, SENS, CELL), P(CELL, None, None, None)),
        out_specs=P(ALL),
        check_vma=False,
    )
```

time: 192 us -> 75.5 us (0.39)
  blocking collectives: 83 us -> 0 us
  Pallas kernels: 0 us -> 74.8 us
  waiting for transfers between devices: 64.8 us -> 0 us
  between operations: 13.5 us -> 0.01 us
  starting transfers between devices: 11.4 us -> 0 us
  local copies, waits for them, and re-layouts: 10.6 us -> 0.56 us
  other arithmetic: 4.06 us -> 0 us
  matrix products: 3.92 us -> 0 us
    pallas_call x0 -> x1, Pallas kernels: none -> 74.8 us  [shards(): pl.pallas_call(kernel, out_shape=pltpu.VMEM((1, cells), jnp.float32), in_...]
    all_gather x1 -> x0, waiting for transfers between devices: 64.8 us -> none  [all_blocks(): parts = lax.all_gather(parts, axes[k])]
    pmax x4 -> x0, blocking collectives: 54.4 us -> none  [one_axis_at_a_time(): return functools.reduce(lax.pmax, axes, value)]
    all_to_all x1 -> x0, blocking collectives: 18 us -> none  [sent_and_summed(): lax.all_to_all(parts, axis, split_axis=0, concat_axis=0, tiled=True)]
    all_to_all x1 -> x0, starting transfers between devices: 11.4 us -> none  [shards(): lax.all_to_all(replicas, SENS, split_axis=0, concat_axis=2, tiled=True)]
    all_gather x1 -> x0, blocking collectives: 10.7 us -> none  [all_blocks(): parts = lax.all_gather(parts, axes[k])]
    dot_general x4 -> x0, matrix products: 3.92 us -> none  [the longest x1 1.86 us: band_power(): jnp.einsum('fst,ftc->fsc', imag_k, real_w, preferred_element_type=jnp.flo...]
    all_to_all x1 -> x0, local copies, waits for them, and re-layouts: 2.71 us -> none  [shards(): lax.all_to_all(replicas, SENS, split_axis=0, concat_axis=2, tiled=True)]
  transfers between devices with their start and end apart: 2 -> 0, of which waited for: 1 -> 0; matrix products, arithmetic and copies ran while one was open for 4% -> 0% of each run, Pallas kernels for 0% -> 0%
where the time goes in v2:
time: 75.5 us; the launch traced here: 75.3 us
  Pallas kernels  74.8 us (99%)
    pallas_call x1, Pallas kernels, shards(): pl.pallas_call(kernel, out_shape=pltpu.VMEM((1, cells), jnp.float32), in_...  74.8 us

profile of v2, /device:TPU:1, one launch (start us, length us, event | category | flops | bytes accessed | tf_op | source)
XLA Modules:
  0.0 75.3 jit_solution(14293095001548710074)
XLA Ops:
  0.0 74.8 %shard_map.28 = f32[1,256]{1,0:T(1,128)S(1)} custom-call(bf16[64,2,8,2048]{3,2,1,0:T(8,128)(2,1)} %waves_hbm.1, f32[1,2,64,64]{3,2,1,0:T(8,128)} %csm_hbm.1), custom_call_target="tpu_custom_call" | custom-call | tf_op jit(solution)/shard_map/pallas_call | solution.py:255
  74.8 0.6 copy.4

commit v3 on v2

--- a/solution.py
+++ b/solution.py
@@ -14,7 +14,8 @@
 ALL = ("cx", "cz", "sy", "sc")
 SIZES = (4, 16, 4, 2)
 
-CHUNKS = (56, 8)
+CHUNKS = (8, 48, 8)
+STAGED = 1
 UNROLL = 8
 LANES = 128
 
@@ -40,6 +41,7 @@
     csm_hbm,
     out_ref,
     csm_vmem,
+    staged,
     waves,
     mats,
     local_sem,
@@ -64,6 +66,13 @@
     csm_in = pltpu.make_async_copy(csm_hbm.at[0], csm_vmem, local_sem.at[0])
     csm_in.start()
 
+    def stage_copy(chunk):
+        part = pl.ds(starts[chunk], CHUNKS[chunk])
+        return pltpu.make_async_copy(waves_hbm.at[part], staged.at[part], local_sem.at[2 + chunk])
+
+    for chunk in range(STAGED):
+        stage_copy(chunk).start()
+
     barrier = pltpu.get_barrier_semaphore()
     greeted = NEAR[1:] + ALONG_X[1:] + [ALONG_Z[1], ALONG_Z[-1]]
     for offset in greeted:
@@ -86,7 +95,7 @@
         i = NEAR.index(offset)
         to = at(offset)
         return pltpu.make_async_remote_copy(
-            src_ref=waves_hbm.at[part, :, :, block(to["sy"] * NC + to["sc"])],
+            src_ref=(staged if chunk < STAGED else waves_hbm).at[part, :, :, block(to["sy"] * NC + to["sc"])],
             dst_ref=waves.at[me, part],
             send_sem=wave_send.at[chunk, i],
             recv_sem=wave_recv.at[chunk, me],
@@ -97,7 +106,7 @@
     def wave_arrival(chunk, s):
         part = pl.ds(starts[chunk], CHUNKS[chunk])
         return pltpu.make_async_remote_copy(
-            src_ref=waves_hbm.at[part, :, :, block(s)],
+            src_ref=(staged if chunk < STAGED else waves_hbm).at[part, :, :, block(s)],
             dst_ref=waves.at[s, part],
             send_sem=wave_send.at[chunk, 0],
             recv_sem=wave_recv.at[chunk, s],
@@ -109,6 +118,8 @@
         return pltpu.make_async_copy(waves_hbm.at[:, :, :, block(me)], waves.at[me], local_sem.at[1])
 
     for chunk in range(len(CHUNKS)):
+        if chunk < STAGED:
+            stage_copy(chunk).wait()
         for offset in far_first(NEAR):
             wave_copy(chunk, offset).start()
     own_copy().start()
@@ -259,9 +270,10 @@
             out_specs=pl.BlockSpec(memory_space=pltpu.VMEM),
             scratch_shapes=[
                 pltpu.VMEM((2, side, side), jnp.float32),
+                pltpu.VMEM((max(1, sum(CHUNKS[:STAGED])), 2, rows, wide), jnp.bfloat16),
                 pltpu.VMEM((NS, freqs, 2, rows, cells), jnp.bfloat16),
                 pltpu.VMEM((NX, NZ, side, 2 * side), jnp.bfloat16),
-                dma((2,)),
+                dma((2 + STAGED,)),
                 dma((len(CHUNKS), NS)),
                 dma((len(CHUNKS), NS)),
                 dma((2, NZ // 2 + 1)),

time: 75.5 us -> 75.4 us (level)
  no operation moved by 1% of the time
where the time goes in v3:
time: 75.4 us; the launch traced here: 75.3 us
  Pallas kernels  74.7 us (99%)
    pallas_call x1, Pallas kernels, shards(): pl.pallas_call(kernel, out_shape=pltpu.VMEM((1, cells), jnp.float32), in_...  74.7 us

profile of v3, /device:TPU:1, one launch (start us, length us, event | category | flops | bytes accessed | tf_op | source)
XLA Modules:
  0.0 75.3 jit_solution(583223058675855191)
XLA Ops:
  0.0 74.7 %shard_map.28 = f32[1,256]{1,0:T(1,128)S(1)} custom-call(bf16[64,2,8,2048]{3,2,1,0:T(8,128)(2,1)} %waves_hbm.1, f32[1,2,64,64]{3,2,1,0:T(8,128)} %csm_hbm.1), custom_call_target="tpu_custom_call" | custom-call | tf_op jit(solution)/shard_map/pallas_call | solution.py:266
  74.7 0.6 copy.4

commit v4 on v3

--- a/solution.py
+++ b/solution.py
@@ -215,7 +215,7 @@
                 src_ref=slots.at[0],
                 dst_ref=slots.at[back],
                 send_sem=send.at[i],
-                recv_sem=recv.at[back],
+                recv_sem=recv,
                 device_id=at(offset),
                 device_id_type=MESH,
             )
@@ -228,17 +228,15 @@
         slots[0] = peak
         for copy in copies:
             copy.start()
-        for offset in far_first(PHASES[phase])[::-1]:
-            i = PHASES[phase].index(offset)
-            _, send, recv = peak_refs[3 * phase : 3 * phase + 3]
-            pltpu.make_async_remote_copy(
-                src_ref=slots.at[0],
-                dst_ref=slots.at[i],
-                send_sem=send.at[i],
-                recv_sem=recv.at[i],
-                device_id=at(offset),
-                device_id_type=MESH,
-            ).wait_recv()
+        arrived = slots.at[pl.ds(1, len(copies))]
+        pltpu.make_async_remote_copy(
+            src_ref=arrived,
+            dst_ref=arrived,
+            send_sem=peak_refs[3 * phase + 1].at[0],
+            recv_sem=peak_refs[3 * phase + 2],
+            device_id=at(PHASES[phase][1]),
+            device_id_type=MESH,
+        ).wait_recv()
         peak = jnp.max(slots[...], axis=0)
     out_ref[...] = total / jnp.max(peak)
 
@@ -262,7 +260,7 @@
         side = csm.shape[-1]
         cells = wide // NS
         dma = pltpu.SemaphoreType.DMA
-        peaks = [s for p in PHASES for s in (pltpu.VMEM((len(p), 1, LANES), jnp.float32), dma((len(p),)), dma((len(p),)))]
+        peaks = [s for p in PHASES for s in (pltpu.VMEM((len(p), 1, LANES), jnp.float32), dma((len(p),)), dma)]
         out = pl.pallas_call(
             kernel,
             out_shape=pltpu.VMEM((1, cells), jnp.float32),

time: 75.4 us -> 75 us (level)
  no operation moved by 1% of the time
where the time goes in v4:
time: 75 us; the launch traced here: 74.9 us
  Pallas kernels  74.3 us (99%)
    pallas_call x1, Pallas kernels, shards(): pl.pallas_call(kernel, out_shape=pltpu.VMEM((1, cells), jnp.float32), in_...  74.3 us

profile of v4, /device:TPU:1, one launch (start us, length us, event | category | flops | bytes accessed | tf_op | source)
XLA Modules:
  0.0 74.9 jit_solution(11759650017108002004)
XLA Ops:
  0.0 74.3 %shard_map.28 = f32[1,256]{1,0:T(1,128)S(1)} custom-call(bf16[64,2,8,2048]{3,2,1,0:T(8,128)(2,1)} %waves_hbm.1, f32[1,2,64,64]{3,2,1,0:T(8,128)} %csm_hbm.1), custom_call_target="tpu_custom_call" | custom-call | tf_op jit(solution)/shard_map/pallas_call | solution.py:264
  74.3 0.6 copy.4

commit v5 on v4

--- a/solution.py
+++ b/solution.py
@@ -210,17 +210,26 @@
         slots, send, recv = peak_refs[3 * phase : 3 * phase + 3]
 
         def copy(offset):
-            i, back = offsets.index(offset), offsets.index(opposite(offset))
+            back = offsets.index(opposite(offset))
             return pltpu.make_async_remote_copy(
                 src_ref=slots.at[0],
                 dst_ref=slots.at[back],
-                send_sem=send.at[i],
+                send_sem=send,
                 recv_sem=recv,
                 device_id=at(offset),
                 device_id_type=MESH,
             )
 
         return slots, [copy(o) for o in far_first(offsets)]
+
+    def sent_before():
+        for chunk in range(len(CHUNKS)):
+            for offset in NEAR[1:]:
+                wave_copy(chunk, offset).wait_send()
+        for way, hop in hops:
+            ring_copy(way, hop).wait_send()
+        for offset in ALONG_X[1:]:
+            x_copy(offset).wait_send()
 
     peak = functools.reduce(jnp.maximum, [total[:, k : k + LANES] for k in range(0, cells, LANES)])
     for phase in range(len(PHASES)):
@@ -228,28 +237,21 @@
         slots[0] = peak
         for copy in copies:
             copy.start()
+        if phase == 0:
+            sent_before()
         arrived = slots.at[pl.ds(1, len(copies))]
-        pltpu.make_async_remote_copy(
+        everyone = pltpu.make_async_remote_copy(
             src_ref=arrived,
             dst_ref=arrived,
-            send_sem=peak_refs[3 * phase + 1].at[0],
+            send_sem=peak_refs[3 * phase + 1],
             recv_sem=peak_refs[3 * phase + 2],
             device_id=at(PHASES[phase][1]),
             device_id_type=MESH,
-        ).wait_recv()
+        )
+        everyone.wait_send()
+        everyone.wait_recv()
         peak = jnp.max(slots[...], axis=0)
     out_ref[...] = total / jnp.max(peak)
-
-    for chunk in range(len(CHUNKS)):
-        for offset in NEAR[1:]:
-            wave_copy(chunk, offset).wait_send()
-    for way, hop in hops:
-        ring_copy(way, hop).wait_send()
-    for offset in ALONG_X[1:]:
-        x_copy(offset).wait_send()
-    for phase in range(len(PHASES)):
-        for copy in peak_copies(phase)[1]:
-            copy.wait_send()
 
 
 def solution(mesh):
@@ -260,7 +262,7 @@
         side = csm.shape[-1]
         cells = wide // NS
         dma = pltpu.SemaphoreType.DMA
-        peaks = [s for p in PHASES for s in (pltpu.VMEM((len(p), 1, LANES), jnp.float32), dma((len(p),)), dma)]
+        peaks = [s for p in PHASES for s in (pltpu.VMEM((len(p), 1, LANES), jnp.float32), dma, dma)]
         out = pl.pallas_call(
             kernel,
             out_shape=pltpu.VMEM((1, cells), jnp.float32),

time: 75 us -> 74.5 us (level)
  no operation moved by 1% of the time
where the time goes in v5:
time: 74.5 us; the launch traced here: 74.3 us
  Pallas kernels  73.8 us (99%)
    pallas_call x1, Pallas kernels, shards(): pl.pallas_call(kernel, out_shape=pltpu.VMEM((1, cells), jnp.float32), in_...  73.8 us

profile of v5, /device:TPU:1, one launch (start us, length us, event | category | flops | bytes accessed | tf_op | source)
XLA Modules:
  0.0 74.3 jit_solution(1975338561224477772)
XLA Ops:
  0.0 73.8 %shard_map.28 = f32[1,256]{1,0:T(1,128)S(1)} custom-call(bf16[64,2,8,2048]{3,2,1,0:T(8,128)(2,1)} %waves_hbm.1, f32[1,2,64,64]{3,2,1,0:T(8,128)} %csm_hbm.1), custom_call_target="tpu_custom_call" | custom-call | tf_op jit(solution)/shard_map/pallas_call | solution.py:266
  73.8 0.6 copy.4

commit v6 on v5

--- a/solution.py
+++ b/solution.py
@@ -14,8 +14,7 @@
 ALL = ("cx", "cz", "sy", "sc")
 SIZES = (4, 16, 4, 2)
 
-CHUNKS = (8, 48, 8)
-STAGED = 1
+CHUNKS = (56, 8)
 UNROLL = 8
 LANES = 128
 
@@ -41,7 +40,6 @@
     csm_hbm,
     out_ref,
     csm_vmem,
-    staged,
     waves,
     mats,
     local_sem,
@@ -66,13 +64,6 @@
     csm_in = pltpu.make_async_copy(csm_hbm.at[0], csm_vmem, local_sem.at[0])
     csm_in.start()
 
-    def stage_copy(chunk):
-        part = pl.ds(starts[chunk], CHUNKS[chunk])
-        return pltpu.make_async_copy(waves_hbm.at[part], staged.at[part], local_sem.at[2 + chunk])
-
-    for chunk in range(STAGED):
-        stage_copy(chunk).start()
-
     barrier = pltpu.get_barrier_semaphore()
     greeted = NEAR[1:] + ALONG_X[1:] + [ALONG_Z[1], ALONG_Z[-1]]
     for offset in greeted:
@@ -95,21 +86,21 @@
         i = NEAR.index(offset)
         to = at(offset)
         return pltpu.make_async_remote_copy(
-            src_ref=(staged if chunk < STAGED else waves_hbm).at[part, :, :, block(to["sy"] * NC + to["sc"])],
+            src_ref=waves_hbm.at[part, :, :, block(to["sy"] * NC + to["sc"])],
             dst_ref=waves.at[me, part],
             send_sem=wave_send.at[chunk, i],
-            recv_sem=wave_recv.at[chunk, me],
+            recv_sem=wave_recv.at[chunk],
             device_id=to,
             device_id_type=MESH,
         )
 
-    def wave_arrival(chunk, s):
+    def wave_arrival(chunk):
         part = pl.ds(starts[chunk], CHUNKS[chunk])
         return pltpu.make_async_remote_copy(
-            src_ref=(staged if chunk < STAGED else waves_hbm).at[part, :, :, block(s)],
-            dst_ref=waves.at[s, part],
+            src_ref=waves.at[pl.ds(0, NS - 1), part],
+            dst_ref=waves.at[pl.ds(0, NS - 1), part],
             send_sem=wave_send.at[chunk, 0],
-            recv_sem=wave_recv.at[chunk, s],
+            recv_sem=wave_recv.at[chunk],
             device_id=at(NEAR[1]),
             device_id_type=MESH,
         )
@@ -118,8 +109,6 @@
         return pltpu.make_async_copy(waves_hbm.at[:, :, :, block(me)], waves.at[me], local_sem.at[1])
 
     for chunk in range(len(CHUNKS)):
-        if chunk < STAGED:
-            stage_copy(chunk).wait()
         for offset in far_first(NEAR):
             wave_copy(chunk, offset).start()
     own_copy().start()
@@ -199,9 +188,7 @@
 
     total = jnp.zeros((1, cells), jnp.float32)
     for chunk, first in enumerate(starts):
-        for offset in far_first(NEAR)[::-1]:
-            s = at(offset)
-            wave_arrival(chunk, s["sy"] * NC + s["sc"]).wait_recv()
+        wave_arrival(chunk).wait_recv()
         count = CHUNKS[chunk]
         total = lax.fori_loop(first, first + count, lambda f, t: t + term(f), total, unroll=min(UNROLL, count))
 
@@ -270,12 +257,11 @@
             out_specs=pl.BlockSpec(memory_space=pltpu.VMEM),
             scratch_shapes=[
                 pltpu.VMEM((2, side, side), jnp.float32),
-                pltpu.VMEM((max(1, sum(CHUNKS[:STAGED])), 2, rows, wide), jnp.bfloat16),
                 pltpu.VMEM((NS, freqs, 2, rows, cells), jnp.bfloat16),
                 pltpu.VMEM((NX, NZ, side, 2 * side), jnp.bfloat16),
-                dma((2 + STAGED,)),
+                dma((2,)),
                 dma((len(CHUNKS), NS)),
-                dma((len(CHUNKS), NS)),
+                dma((len(CHUNKS),)),
                 dma((2, NZ // 2 + 1)),
                 dma((2, NZ // 2 + 1)),
                 dma((NX,)),

time: 74.5 us -> 74.4 us (level)
  no operation moved by 1% of the time
where the time goes in v6:
time: 74.4 us; the launch traced here: 74.3 us
  Pallas kernels  73.7 us (99%)
    pallas_call x1, Pallas kernels, shards(): pl.pallas_call(kernel, out_shape=pltpu.VMEM((1, cells), jnp.float32), in_...  73.7 us

profile of v6, /device:TPU:1, one launch (start us, length us, event | category | flops | bytes accessed | tf_op | source)
XLA Modules:
  0.0 74.3 jit_solution(13200349165198962271)
XLA Ops:
  0.0 73.7 %shard_map.28 = f32[1,256]{1,0:T(1,128)S(1)} custom-call(bf16[64,2,8,2048]{3,2,1,0:T(8,128)(2,1)} %waves_hbm.1, f32[1,2,64,64]{3,2,1,0:T(8,128)} %csm_hbm.1), custom_call_target="tpu_custom_call" | custom-call | tf_op jit(solution)/shard_map/pallas_call | solution.py:253
  73.7 0.6 copy.4
